TPU v7x, 256 devices: a 4x2x16 block of a 4x16x16 slice. The times are simulated.
256 devices in a mesh: groups: 2 (over y), gx: 32 (over z, core), gy: 4 (over x).
Axes of the slice: x: 4, y: 2, z: 16, core: 2. Of those that a mesh axis runs over, the one named last changes fastest.
The devices are a block of a 4x16x16 slice.
Arguments:
- hidden_in: bfloat16 [1024, 18432], P(('groups', 'gx'), 'gy'), parts along dimension 0, may hold values from -6 to 6
- w_query: bfloat16 [18432, 12288], P('gy', 'gx'), may hold values from -0.046875 to 0.046875
- w_out: bfloat16 [12288, 18432], P('gx', 'gy'), may hold values from -0.4375 to 0.4375
- cache_keys: bfloat16 [1024, 1024, 256], P(('groups', 'gx', 'gy')), parts along dimension 0, may hold values from -250 to 250
- cache_values: bfloat16 [1024, 1024, 256], P(('groups', 'gx', 'gy')), parts along dimension 0, may hold values from -6 to 6
- lengths: int32 [1024], P(('groups', 'gx', 'gy')), parts along dimension 0, may hold values from 128 to 1024
Outputs:
- layer_out: bfloat16 [1024, 18432], P(('groups', 'gx'), 'gy'), parts along dimension 0
There are 2 independent parts, one for each index of `groups`. A program takes and returns all parts, laid end to end along the dimension named above; an argument that names none is the same for every part. Nothing has to cross between parts.
All inputs are finite; a program needn't handle non-finite values.
Results may differ from a plain program's by a relative error of at most 0.0097.
Values may be sent and summed in bfloat16 or wider, within the bound.
A program may use at most 64 MiB of HBM per device.

v0:
```python
import jax
import jax.numpy as jnp
from jax import lax
from jax.sharding import Mesh
from jax.sharding import PartitionSpec as P

GX = ("gx_0", "gx_1")
GROUPS_GX = ("groups", "gx_0", "gx_1")
GROUPS_GX_GY = ("groups", "gx_0", "gx_1", "gy")


def cut_along(x, dim, size):
    dims = x.shape
    tiles = x.reshape(*dims[:dim], size, dims[dim] // size, *dims[dim + 1 :])
    return jnp.moveaxis(tiles, dim, 0)


def summed_on_arrival(x, axis, dim):
    size = lax.axis_size(axis)
    tiles = lax.all_to_all(cut_along(x, dim, size), axis, 0, 0, tiled=True)
    return jnp.sum(tiles, axis=0)


def reduced_to_own(tiles, axes, sequence):
    dims = [lax.axis_size(a) for a in axes]
    tiles = tiles.reshape(*dims, *tiles.shape[1:])
    tiles = tiles.transpose(*sequence, *range(len(axes), tiles.ndim))
    tiles = tiles.reshape(-1, *tiles.shape[len(axes) :])
    for k in sequence:
        tiles = lax.psum_scatter(tiles, axes[k], scatter_dimension=0, tiled=True)
    return tiles[0]


def sum_by_axis(x, axes, sequence, dim):
    size = lax.axis_size(axes)
    return reduced_to_own(cut_along(x, dim, size), axes, sequence)


def body(hidden_in, w_query, w_out, cache_keys, cache_values, lengths):
    across = lax.axis_size(GX)
    within = lax.axis_size("gy")
    local_seqs = cache_keys.shape[0]
    slot_count = cache_keys.shape[1]
    head_dim = cache_keys.shape[2]
    partial_query = jnp.dot(
        lax.all_gather(hidden_in, GX, axis=0, tiled=True),
        w_query,
        preferred_element_type=jnp.float32,
    )
    slice_width = partial_query.shape[1]
    grouped = partial_query.reshape(across, within, local_seqs, slice_width)
    own_rows = summed_on_arrival(grouped, "gy", 1)
    query_rows = own_rows.reshape(across * local_seqs, slice_width).astype(jnp.bfloat16)
    query = lax.all_to_all(query_rows, GX, split_axis=0, concat_axis=1, tiled=True)
    head_count = query.shape[1] // head_dim
    query_heads = query.reshape(local_seqs, head_count, head_dim)
    scores = jnp.einsum("bhd,bld->bhl", query_heads, cache_keys, preferred_element_type=jnp.float32)
    scores = scores / jnp.sqrt(jnp.float32(head_dim))
    live_slots = jnp.arange(slot_count)[None, None, :] < lengths[:, None, None]
    scores = jnp.where(live_slots, scores, jnp.float32(-1e30))
    top_score = jnp.max(scores, axis=2, keepdims=True)
    expo = jnp.where(live_slots, jnp.exp(scores - top_score), jnp.float32(0.0))
    probs = (expo / jnp.sum(expo, axis=2, keepdims=True)).astype(jnp.bfloat16)
    mixed = jnp.einsum("bhl,bld->bhd", probs, cache_values, preferred_element_type=jnp.float32)
    attended = mixed.astype(jnp.bfloat16).reshape(local_seqs, head_count * head_dim)
    spread = lax.all_to_all(attended, GX, split_axis=1, concat_axis=0, tiled=True)
    stacked = spread.reshape(across, local_seqs, slice_width)
    gathered = lax.all_gather(stacked, "gy", axis=1, tiled=True)
    head_rows = gathered.reshape(across * within * local_seqs, slice_width)
    result = sum_by_axis(
        jnp.dot(head_rows, w_out, preferred_element_type=jnp.float32), GX, (1, 0), 0
    )
    return result.astype(jnp.bfloat16)


def solution(mesh):
    torus = Mesh(
        mesh.devices.reshape(mesh.shape["groups"], 16, 2, mesh.shape["gy"]),
        ("groups", "gx_0", "gx_1", "gy"),
    )
    placed = (
        P(GROUPS_GX, "gy"),
        P("gy", GX),
        P(GX, "gy"),
        P(GROUPS_GX_GY, None, None),
        P(GROUPS_GX_GY, None, None),
        P(GROUPS_GX_GY),
    )
    return jax.shard_map(
        body, mesh=torus, in_specs=placed, out_specs=P(GROUPS_GX, "gy"), check_vma=False
    )
```

profile of v0, /device:TPU:36, one launch (start us, length us, event | category | flops | bytes accessed | tf_op | source)
XLA Modules:
  0.0 308.4 jit_solution(460804432666121327)
XLA Ops:
  6.5 0.0 copy-start
  6.6 0.0 all-gather.2.cloned.1.call-start
  6.6 0.7 all-gather.2.cloned.1.call-update
  7.3 87.8 %all-gather.2.cloned.1.call-done = bf16[512,4608]{1,0:T(8,128)(2,1)} async-done(((bf16[16,4608]{1,0:T(8,128)(2,1)}), bf16[512,4608]{1,0:T(8,128)(2,1)}) %all-gather.2.cloned.1.call-update) | async-done | bytes 4718608 | tf_op jit(solution)/shard_map/all_gather | solution.py:46
  95.1 6.9 %fusion.10 = f32[512,384]{1,0:T(8,128)} fusion(bf16[512,4608]{1,0:T(8,128)(2,1)} %all-gather.2.cloned.1.call-done, bf16[4608,384]{1,0:T(8,128)(2,1)} %param.7), kind=kOutput, calls=%fused_computation.17 | convolution fusion | flops 1811939328 | bytes 9043968 | tf_op jit(solution)/shard_map/dot_general | solution.py:45
  102.0 2.2 reshape_reshape.4
  104.2 1.2 copy.20
  105.5 14.7 %all_to_all.34 = f32[4,32,1,4,384]{4,3,1,2,0:T(4,128)} all-to-all(f32[4,32,1,4,384]{4,3,1,2,0:T(4,128)S(1)} %bitcast.25), channel_id=1, replica_groups=mesh['groups'=2,'gx_0'=16,'gx_1'=2,'gy'=4] {'gy'}, dimensions={0} | all-to-all | bytes 1572864 | tf_op jit(solution)/shard_map/all_to_all | solution.py:20
  120.1 2.0 reduce_sum.18
  122.1 8.8 %all-to-all-start.1 = ((bf16[32,4,384]{2,1,0:T(4,128)(2,1)}), bf16[32,4,384]{2,1,0:T(4,128)(2,1)}, u32[]{:S(2)}, u32[]{:S(2)}) async-start(bf16[32,4,384]{2,1,0:T(4,128)(2,1)} %reduce_sum.18), calls=%async_computation.1 | async-start | bytes 196608 | tf_op jit(solution)/shard_map/all_to_all | solution.py:54
  130.9 0.1 reduce-scatter.3.cloned.1.call-start
  131.0 0.1 iota_compare_fusion
  131.1 15.0 %all-to-all-done.1 = bf16[32,4,384]{2,1,0:T(4,128)(2,1)} async-done(((bf16[32,4,384]{2,1,0:T(4,128)(2,1)}), bf16[32,4,384]{2,1,0:T(4,128)(2,1)}, u32[]{:S(2)}, u32[]{:S(2)}) %all-to-all-start.1) | async-done | bytes 98336 | tf_op jit(solution)/shard_map/all_to_all | solution.py:54
  146.1 1.5 copy.12
  147.6 1.6 reshape.48
  149.2 2.4 fusion.5
  151.6 0.9 copy-done.1
  152.5 0.3 fusion.9
  152.8 3.2 %convolution_convert_fusion = bf16[4,48,256]{2,1,0:T(8,128)(2,1)} fusion(bf16[4,1024,256]{2,1,0:T(8,128)(2,1)} %param.10, f32[4,48]{1,0:T(4,128)S(1)} %fusion.9, f32[4,48,1024]{2,1,0:T(8,128)} %copy-done.1, pred[4,1024]{1,0:T(4,128)(4,1)S(1)} %iota_compare_fusion), kind=kOutput, calls=%fused_computation.8 | convolution fusion | flops 101500096 | bytes 2986752 | tf_op jit(solution)/shard_map/bhl,bld->bhd/dot_general | solution.py:64
  156.0 1.6 all_to_all.28
  157.6 0.9 copy.13
  158.6 18.9 %all_to_all.35 = bf16[4,32,384]{2,0,1:T(4,128)(2,1)S(1)} all-to-all(bf16[4,32,384]{2,0,1:T(4,128)(2,1)S(1)} %copy.13), channel_id=1, replica_groups=mesh['groups'=2,'gx_0'=16,'gx_1'=2,'gy'=4] {'gx_0','gx_1'}, dimensions={1} | all-to-all | bytes 196608 | tf_op jit(solution)/shard_map/all_to_all | solution.py:66
  177.5 13.6 %all_gather.7 = bf16[32,16,384]{2,0,1:T(8,128)(2,1)S(1)} all-gather(bf16[32,4,384]{2,0,1:T(8,128)(2,1)S(1)} %copy.14), channel_id=1, replica_groups=mesh['groups'=2,'gx_0'=16,'gx_1'=2,'gy'=4] {'gy'}, dimensions={1}, use_global_device_ids=true | all-gather | bytes 491520 | tf_op jit(solution)/shard_map/all_gather | solution.py:68
  191.1 0.1 copy.15
  191.2 2.6 convolution_bitcast_fusion
  193.8 4.2 %copy.16 = f32[2,16,16,4608]{3,2,1,0:T(8,128)} copy(f32[2,16,16,4608]{3,2,0,1:T(8,128)S(1)} %convolution_bitcast_fusion) | data formatting | bytes 18874368 | tf_op jit(solution)/shard_map/transpose | solution.py:27
  198.1 0.1 reduce-scatter.3.cloned.1.call-update
  198.2 0.1 reduce-scatter.5.cloned.1.call-start
  198.2 17.6 %reduce-scatter.3.cloned.1.call-done = f32[16,16,4608]{2,1,0:T(8,128)} async-done(((f32[32,16,4608]{2,1,0:T(8,128)}), f32[16,16,4608]{2,1,0:T(8,128)}) %reduce-scatter.3.cloned.1.call-update) | async-done | bytes 4718608 | tf_op jit(solution)/shard_map/reduce_scatter | solution.py:30
  215.8 0.1 reduce-scatter.5.cloned.1.call-update
  215.9 84.3 %reduce-scatter.5.cloned.1.call-done = f32[1,16,4608]{2,1,0:T(8,128)} async-done(((f32[16,16,4608]{2,1,0:T(8,128)}), f32[1,16,4608]{2,1,0:T(8,128)}) %reduce-scatter.5.cloned.1.call-update) | async-done | bytes 294928 | tf_op jit(solution)/shard_map/reduce_scatter | solution.py:30
  300.2 1.6 convert_bitcast_fusion
  (5 shorter events, 0.0 us)
Async XLA Ops:
  6.5 184.7 %copy-start = (bf16[384,4608]{1,0:T(8,128)(2,1)S(1)}, bf16[384,4608]{1,0:T(8,128)(2,1)}, u32[]{:S(2)}) copy-start(bf16[384,4608]{1,0:T(8,128)(2,1)} %param.8) | copy-start | bytes 10616836
  6.6 88.5 %all-gather.2.cloned.1.call-start = ((), (), s32[]{:S(2)}) async-start(), calls=%async_computation.5 | async-start | bytes 4866048 | tf_op jit(solution)/shard_map/all_gather | solution.py:46
  102.0 29.0 %copy-start.2 = (s32[4]{0:T(128)S(1)}, s32[4]{0:T(128)}, u32[]{:S(2)}) copy-start(s32[4]{0:T(128)} %param.11) | copy-start | bytes 52
  122.1 24.0 %all-to-all-start.1 = ((bf16[32,4,384]{2,1,0:T(4,128)(2,1)}), bf16[32,4,384]{2,1,0:T(4,128)(2,1)}, u32[]{:S(2)}, u32[]{:S(2)}) async-start(bf16[32,4,384]{2,1,0:T(4,128)(2,1)} %reduce_sum.18), calls=%async_computation.1 | async-start | bytes 196608 | tf_op jit(solution)/shard_map/all_to_all | solution.py:54
  130.9 84.9 %reduce-scatter.3.cloned.1.call-start = ((), (), s32[]{:S(2)}) async-start(), calls=%async_computation.6 | async-start | bytes 14155776 | tf_op jit(solution)/shard_map/reduce_scatter | solution.py:30
  151.6 0.9 copy-start.1
  198.2 102.1 %reduce-scatter.5.cloned.1.call-start = ((), (), s32[]{:S(2)}) async-start(), calls=%async_computation.7 | async-start | bytes 5013504 | tf_op jit(solution)/shard_map/reduce_scatter | solution.py:30
Sparse Core Ops, SparseCore 0:
  9.2 85.8 all-gather.1
  198.3 17.4 reduce-scatter.2
  218.4 81.7 reduce-scatter.4
where the time goes:
time: 309 us; the launch traced here: 308 us
  waiting for transfers between devices  206 us (67%)
  blocking collectives  47.2 us (15%)
  matrix products  15.2 us (5%)
  local copies, waits for them, and re-layouts  14.4 us (5%)
  between operations  13.2 us (4%)
  starting transfers between devices  8.93 us (3%)
  other arithmetic  3.99 us (1%)
    reduce_scatter x2, waiting for transfers between devices, reduced_to_own(): tiles = lax.psum_scatter(tiles, axes[k], scatter_dimension=0, tiled=True)  102 us
    all_gather x1, waiting for transfers between devices, body(): lax.all_gather(hidden_in, GX, axis=0, tiled=True)  87.8 us
    all_to_all x1, blocking collectives, body(): lax.all_to_all(attended, GX, split_axis=1, concat_axis=0, tiled=True)  18.9 us
    all_to_all x1, waiting for transfers between devices, body(): lax.all_to_all(query_rows, GX, split_axis=0, concat_axis=1, tiled=True)  15 us
    all_to_all x1, blocking collectives, summed_on_arrival(): tiles = lax.all_to_all(cut_along(x, dim, size), axis, 0, 0, tiled=True)  14.7 us
    all_gather x1, blocking collectives, body(): gathered = lax.all_gather(stacked, 'gy', axis=1, tiled=True)  13.6 us
    all_to_all x1, starting transfers between devices, body(): lax.all_to_all(query_rows, GX, split_axis=0, concat_axis=1, tiled=True)  8.8 us
    dot_general x1, matrix products, body(): jnp.dot(lax.all_gather(hidden_in, GX, axis=0, tiled=True), w_query, prefe...  6.93 us
  transfers between devices with their start and end apart: 4, of which 4 were waited for; matrix products, arithmetic and copies ran while one was open for 0% of the time, Pallas kernels for 0%

commit v1 on v0

--- a/solution.py
+++ b/solution.py
@@ -43,7 +43,9 @@
     slot_count = cache_keys.shape[1]
     head_dim = cache_keys.shape[2]
     partial_query = jnp.dot(
-        lax.all_gather(hidden_in, GX, axis=0, tiled=True),
+        jnp.concatenate(
+            lax.all_to_all(jnp.stack([hidden_in] * lax.axis_size(GX)), GX, 0, 0), axis=0
+        ),
         w_query,
         preferred_element_type=jnp.float32,
     )

time: 309 us -> 453 us (1.47)
  blocking collectives: 47.2 us -> 285 us
  waiting for transfers between devices: 206 us -> 117 us
    all_to_all x0 -> x1, blocking collectives: none -> 237 us  [body(): lax.all_to_all(jnp.stack([hidden_in] * lax.axis_size(GX)), GX, 0, 0)]
    all_gather x1 -> x0, waiting for transfers between devices: 87.8 us -> none  [body(): lax.all_gather(hidden_in, GX, axis=0, tiled=True)]
  transfers between devices with their start and end apart: 4 -> 3, of which waited for: 4 -> 3; matrix products, arithmetic and copies ran while one was open for 0% -> 0% of each run, Pallas kernels for 0% -> 0%
where the time goes in v1:
time: 453 us; the launch traced here: 452 us
  blocking collectives  285 us (63%)
  waiting for transfers between devices  117 us (26%)
  local copies, waits for them, and re-layouts  16.7 us (4%)
  between operations  13.5 us (3%)
  matrix products  10.8 us (2%)
  starting transfers between devices  5.51 us (1%)
    all_to_all x1, blocking collectives, body(): lax.all_to_all(jnp.stack([hidden_in] * lax.axis_size(GX)), GX, 0, 0)  237 us
    reduce_scatter x2, waiting for transfers between devices, reduced_to_own(): tiles = lax.psum_scatter(tiles, axes[k], scatter_dimension=0, tiled=True)  102 us
    all_to_all x1, blocking collectives, body(): lax.all_to_all(attended, GX, split_axis=1, concat_axis=0, tiled=True)  18.9 us
    all_to_all x1, waiting for transfers between devices, body(): lax.all_to_all(query_rows, GX, split_axis=0, concat_axis=1, tiled=True)  14.9 us
    all_to_all x1, blocking collectives, summed_on_arrival(): tiles = lax.all_to_all(cut_along(x, dim, size), axis, 0, 0, tiled=True)  14.5 us
    all_gather x1, blocking collectives, body(): gathered = lax.all_gather(stacked, 'gy', axis=1, tiled=True)  13.8 us
  transfers between devices with their start and end apart: 3, of which 3 were waited for; matrix products, arithmetic and copies ran while one was open for 0% of the time, Pallas kernels for 0%

profile of v1, /device:TPU:36, one launch (start us, length us, event | category | flops | bytes accessed | tf_op | source)
XLA Modules:
  0.0 452.4 jit_solution(3791627587275040087)
XLA Ops:
  6.6 1.6 stack.2
  8.1 237.5 %all_to_all.39 = bf16[32,16,4608]{2,1,0:T(8,128)(2,1)S(1)} all-to-all(bf16[32,16,4608]{2,1,0:T(8,128)(2,1)S(1)} %stack.2), channel_id=1, replica_groups=mesh['groups'=2,'gx_0'=16,'gx_1'=2,'gy'=4] {'gx_0','gx_1'}, dimensions={0} | all-to-all | bytes 9437184 | tf_op jit(solution)/shard_map/all_to_all | solution.py:47
  245.6 2.6 copy.17
  248.2 0.0 copy-start.2
  248.2 2.6 fusion.5
  250.8 14.5 %all_to_all.40 = f32[4,32,1,4,384]{4,1,3,2,0:T(8,128)} all-to-all(f32[4,32,1,4,384]{4,1,3,2,0:T(8,128)S(1)} %fusion.5), channel_id=1, replica_groups=mesh['groups'=2,'gx_0'=16,'gx_1'=2,'gy'=4] {'gy'}, dimensions={0} | all-to-all | bytes 1572864 | tf_op jit(solution)/shard_map/all_to_all | solution.py:20
  265.3 1.8 reduce_sum.18
  267.1 1.6 copy.19
  268.7 5.4 %all-to-all-start.2 = ((bf16[32,4,384]{2,1,0:T(4,128)(2,1)}), bf16[32,4,384]{2,1,0:T(4,128)(2,1)}, u32[]{:S(2)}, u32[]{:S(2)}) async-start(bf16[32,4,384]{2,1,0:T(4,128)(2,1)} %copy.19), calls=%async_computation.2 | async-start | bytes 196608 | tf_op jit(solution)/shard_map/all_to_all | solution.py:56
  274.1 0.1 reduce-scatter.3.cloned.1.call-start
  274.2 0.0 copy-done.2
  274.2 0.1 iota_compare_fusion
  274.3 14.9 %all-to-all-done.2 = bf16[32,4,384]{2,1,0:T(4,128)(2,1)} async-done(((bf16[32,4,384]{2,1,0:T(4,128)(2,1)}), bf16[32,4,384]{2,1,0:T(4,128)(2,1)}, u32[]{:S(2)}, u32[]{:S(2)}) %all-to-all-start.2) | async-done | bytes 98336 | tf_op jit(solution)/shard_map/all_to_all | solution.py:56
  289.2 1.5 copy.20
  290.7 1.6 reshape.59
  292.3 2.4 fusion.10
  294.7 0.9 copy-done.1
  295.6 0.3 fusion.14
  295.9 3.2 convolution_convert_fusion
  299.1 1.6 all_to_all.32
  300.7 0.9 copy.21
  301.7 18.9 %all_to_all.41 = bf16[4,32,384]{2,0,1:T(4,128)(2,1)S(1)} all-to-all(bf16[4,32,384]{2,0,1:T(4,128)(2,1)S(1)} %copy.21), channel_id=1, replica_groups=mesh['groups'=2,'gx_0'=16,'gx_1'=2,'gy'=4] {'gx_0','gx_1'}, dimensions={1} | all-to-all | bytes 196608 | tf_op jit(solution)/shard_map/all_to_all | solution.py:68
  320.5 13.8 %all_gather.3 = bf16[32,16,384]{2,0,1:T(8,128)(2,1)S(1)} all-gather(bf16[32,4,384]{2,0,1:T(8,128)(2,1)S(1)} %copy.22), channel_id=1, replica_groups=mesh['groups'=2,'gx_0'=16,'gx_1'=2,'gy'=4] {'gy'}, dimensions={1}, use_global_device_ids=true | all-gather | bytes 491520 | tf_op jit(solution)/shard_map/all_gather | solution.py:70
  334.3 0.1 copy.23
  334.5 2.6 convolution_bitcast_fusion
  337.1 4.2 copy.24
  341.3 0.1 reduce-scatter.3.cloned.1.call-update
  341.4 0.1 reduce-scatter.5.cloned.1.call-start
  341.5 18.2 %reduce-scatter.3.cloned.1.call-done = f32[16,16,4608]{2,1,0:T(8,128)} async-done(((f32[32,16,4608]{2,1,0:T(8,128)}), f32[16,16,4608]{2,1,0:T(8,128)}) %reduce-scatter.3.cloned.1.call-update) | async-done | bytes 4718608 | tf_op jit(solution)/shard_map/reduce_scatter | solution.py:30
  359.7 0.1 reduce-scatter.5.cloned.1.call-update
  359.7 84.1 %reduce-scatter.5.cloned.1.call-done = f32[1,16,4608]{2,1,0:T(8,128)} async-done(((f32[16,16,4608]{2,1,0:T(8,128)}), f32[1,16,4608]{2,1,0:T(8,128)}) %reduce-scatter.5.cloned.1.call-update) | async-done | bytes 294928 | tf_op jit(solution)/shard_map/reduce_scatter | solution.py:30
  443.9 1.6 convert_bitcast_fusion
  (6 shorter events, 0.0 us)
Async XLA Ops:
  6.5 327.9 %copy-start = (bf16[384,4608]{1,0:T(8,128)(2,1)S(1)}, bf16[384,4608]{1,0:T(8,128)(2,1)}, u32[]{:S(2)}) copy-start(bf16[384,4608]{1,0:T(8,128)(2,1)} %param.8) | copy-start | bytes 10616836
  245.6 2.6 copy-start.3
  248.2 25.9 %copy-start.2 = (s32[4]{0:T(128)S(1)}, s32[4]{0:T(128)}, u32[]{:S(2)}) copy-start(s32[4]{0:T(128)} %param.11) | copy-start | bytes 52
  268.7 20.5 %all-to-all-start.2 = ((bf16[32,4,384]{2,1,0:T(4,128)(2,1)}), bf16[32,4,384]{2,1,0:T(4,128)(2,1)}, u32[]{:S(2)}, u32[]{:S(2)}) async-start(bf16[32,4,384]{2,1,0:T(4,128)(2,1)} %copy.19), calls=%async_computation.2 | async-start | bytes 196608 | tf_op jit(solution)/shard_map/all_to_all | solution.py:56
  274.1 85.6 %reduce-scatter.3.cloned.1.call-start = ((), (), s32[]{:S(2)}) async-start(), calls=%async_computation.6 | async-start | bytes 14155776 | tf_op jit(solution)/shard_map/reduce_scatter | solution.py:30
  294.7 0.9 copy-start.1
  341.4 102.5 %reduce-scatter.5.cloned.1.call-start = ((), (), s32[]{:S(2)}) async-start(), calls=%async_computation.7 | async-start | bytes 5013504 | tf_op jit(solution)/shard_map/reduce_scatter | solution.py:30
Sparse Core Ops, SparseCore 0:
  341.5 18.1 reduce-scatter.2
  362.3 81.5 reduce-scatter.4
